TPU v7x, 32 devices: a 4x2x2 block of a 4x4x8 slice. The times are simulated.
32 devices in a mesh: dp: 4 (over y, z), ep: 8 (over x, core).
Axes of the slice: x: 4, y: 2, z: 2, core: 2. Of those that a mesh axis runs over, the one named last changes fastest.
The devices are a block of a 4x4x8 slice.
Arguments:
- tok_x: bfloat16 [8192, 1536], P(('dp', 'ep')), parts along dimension 0
- expert_ids: int32 [8192, 8], P(('dp', 'ep')), parts along dimension 0
- gates: float32 [8192, 8], P(('dp', 'ep')), parts along dimension 0
- hot_tok: int32 [2048], P(('dp', 'ep')), parts along dimension 0
- hot_gates: float32 [2048], P(('dp', 'ep')), parts along dimension 0
- w_gate: bfloat16 [40, 1536, 512], P('ep')
- w_up: bfloat16 [40, 1536, 512], P('ep')
- w_down: bfloat16 [40, 512, 1536], P('ep')
Outputs:
- output: bfloat16 [8192, 1536], P(('dp', 'ep')), parts along dimension 0
There are 4 independent parts. A program takes and returns all parts, laid end to end along the dimension named above; an argument that names none is the same for every part.
All inputs are finite; a program needn't handle non-finite values.
Results may differ from a plain program's by a relative error of at most 0.00782016.
Values are sent between devices in bfloat16 or wider.
A program may use at most 768 MiB of HBM per device.

v0:
```python
import jax
import jax.numpy as jnp
from jax import lax
from jax.sharding import PartitionSpec as P


def route_plan(flat_ids, num_experts, cold_cap):
    routes = flat_ids.shape[0]
    sort_order = jnp.argsort(flat_ids, stable=True)
    exp_counts = jnp.bincount(flat_ids, length=num_experts).astype(jnp.int32)
    exp_starts = jnp.cumsum(exp_counts) - exp_counts
    slot_pos = jnp.arange(cold_cap, dtype=jnp.int32)
    filled = slot_pos[None, :] < exp_counts[:, None]
    sorted_pos = jnp.minimum(exp_starts[:, None] + slot_pos[None, :], routes - 1)
    src_route = sort_order[sorted_pos]
    route_rank = jnp.zeros((routes,), jnp.int32).at[sort_order].set(jnp.arange(routes, dtype=jnp.int32))
    route_slot = flat_ids * cold_cap + route_rank - exp_starts[flat_ids]
    return src_route, filled, route_slot


def swiglu_rows(in_rows, w_gate_e, w_up_e, w_down_e):
    gate_act = jnp.einsum('...d,df->...f', in_rows, w_gate_e, preferred_element_type=jnp.float32)
    up_act = jnp.einsum('...d,df->...f', in_rows, w_up_e, preferred_element_type=jnp.float32)
    hidden = (jax.nn.silu(gate_act) * up_act).astype(jnp.bfloat16)
    return jnp.einsum('...f,fd->...d', hidden, w_down_e, preferred_element_type=jnp.float32).astype(jnp.bfloat16)


def combine_rows(out_rows, route_slot, gates_loc, hot_loc, hot_g_loc):
    num_tokens, top_k = gates_loc.shape
    hot_count = hot_loc.shape[0]
    cold_total = out_rows.shape[0] - hot_count
    hot_index = jnp.zeros((num_tokens,), jnp.int32).at[hot_loc].set(jnp.arange(hot_count, dtype=jnp.int32))
    hot_weight = jnp.zeros((num_tokens,), jnp.float32).at[hot_loc].set(hot_g_loc)
    all_slots = jnp.concatenate([route_slot.reshape(num_tokens, top_k), (cold_total + hot_index)[:, None]], axis=1)
    all_gates = jnp.concatenate([gates_loc, hot_weight[:, None]], axis=1)
    picked = out_rows[all_slots]
    return jnp.einsum('tk,tkd->td', all_gates, picked, preferred_element_type=jnp.float32).astype(jnp.bfloat16)


def solution(mesh):
    group_size = mesh.shape['ep']
    row_spec = P(('dp', 'ep'), None)
    list_spec = P(('dp', 'ep'))
    expert_spec = P('ep', None, None)

    def local_layer(x_loc, ids_loc, gates_loc, hot_loc, hot_g_loc, wg_loc, wu_loc, wd_loc):
        local_experts = wg_loc.shape[0]
        d_model = x_loc.shape[1]
        num_experts = local_experts * group_size
        num_tokens, top_k = ids_loc.shape
        cold_cap = (num_tokens * top_k + num_experts - 2) // (num_experts - 1)
        block_rows = local_experts * cold_cap
        src_route, filled, route_slot = route_plan(ids_loc.reshape(num_tokens * top_k), num_experts, cold_cap)
        cold_buf = jnp.where(filled[:, :, None], x_loc[src_route // top_k], 0)
        hot_buf = x_loc[hot_loc]
        to_owner = jnp.where(jnp.arange(group_size)[:, None, None] == 0, hot_buf[None], 0)
        send_buf = jnp.concatenate([cold_buf.reshape(group_size, block_rows, d_model), to_owner], axis=1)
        recv_buf = lax.all_to_all(send_buf, 'ep', 0, 0, tiled=True)
        cold_in = recv_buf[:, :block_rows].reshape(group_size, local_experts, cold_cap, d_model)
        gate_act = jnp.einsum('slcd,ldf->slcf', cold_in, wg_loc, preferred_element_type=jnp.float32)
        up_act = jnp.einsum('slcd,ldf->slcf', cold_in, wu_loc, preferred_element_type=jnp.float32)
        hidden = (jax.nn.silu(gate_act) * up_act).astype(jnp.bfloat16)
        cold_out = jnp.einsum('slcf,lfd->slcd', hidden, wd_loc, preferred_element_type=jnp.float32).astype(jnp.bfloat16)
        hot_out = lax.cond(lax.axis_index('ep') == 0,
                           lambda hot_in: swiglu_rows(hot_in, wg_loc[0], wu_loc[0], wd_loc[0]),
                           jnp.zeros_like, recv_buf[:, block_rows:])
        back_buf = jnp.concatenate([cold_out.reshape(group_size, block_rows, d_model), hot_out], axis=1)
        ret_buf = lax.all_to_all(back_buf, 'ep', 0, 0, tiled=True)
        out_rows = jnp.concatenate([ret_buf[:, :block_rows].reshape(num_experts * cold_cap, d_model),
                                    ret_buf[0, block_rows:]], axis=0)
        return combine_rows(out_rows, route_slot, gates_loc, hot_loc, hot_g_loc)

    return jax.shard_map(local_layer, mesh=mesh,
                         in_specs=(row_spec, row_spec, row_spec, list_spec, list_spec, expert_spec, expert_spec, expert_spec),
                         out_specs=row_spec, check_vma=False)
```

profile of v0, /device:TPU:81, one launch (start us, length us, event | category | flops | bytes accessed | tf_op | source)
XLA Modules:
  0.0 388.1 jit_solution(3938703956218461660)
XLA Ops:
  0.0 0.0 copy-start
  0.0 0.9 copy.18
  0.9 0.1 reshape.298
  1.0 0.1 reshape.297
  1.1 0.7 compare_select_fusion.11
  1.8 0.1 lt.81
  1.9 14.7 %scatter_custom_fusion.1 = s32[40]{0:T(128)S(1)} fusion(s32[2048]{0:T(1024)S(1)} %bitcast.129, s32[2048]{0:T(1024)S(1)} %broadcast.280, s32[]{:T(128)} %constant.21.clone.1), kind=kCustom, calls=%fused_computation.115 | custom fusion | flops 2048 | bytes 164 | tf_op jit(solution)/shard_map/scatter-add | solution.py:10
  16.6 0.1 lt.83
  16.7 0.1 copy.20
  16.8 0.1 reduce-window.9
  16.8 0.1 reduce
  17.0 0.1 compare_select_fusion.1
  17.0 0.1 reshape.306
  17.2 5.0 %sort.17 = (s32[2048]{0:T(1024)}, s32[2048]{0:T(1024)S(1)}) sort(s32[2048]{0:T(1024)S(1)} %reshape.298, s32[2048]{0:T(1024)S(1)} %iota.26), dimensions={0}, to_apply=%region_2.3 | sort | flops 22528 | bytes 32768 | tf_op jit(solution)/shard_map/jit(argsort)/sort | solution.py:9
  22.2 11.7 %gather_fusion = s32[2120]{0:T(1024)S(1)} fusion(s32[2048]{0:T(1024)S(1)} %get-tuple-element.21, s32[3072]{0:T(1024)S(1)} %pad_clamp_fusion.2), kind=kCustom, calls=%fused_computation | custom fusion | bytes 25440 | tf_op jit(solution)/shard_map/gather | solution.py:15
  33.9 0.1 gather.20
  34.1 0.1 reshape.314
  34.2 0.1 lt.84
  34.3 0.1 lt.85
  34.3 0.0 copy-done
  34.3 0.7 gather_fusion.2
  35.1 8.6 %gather_fusion.1 = bf16[2120,1536]{1,0:T(8,128)(2,1)} fusion(bf16[256,1536]{1,0:T(8,128)(2,1)S(1)} %copy-done, s32[3072]{0:T(1024)S(1)} %pad_clamp_fusion.1), kind=kCustom, calls=%fused_computation.1 | custom fusion | bytes 13033760 | tf_op jit(solution)/shard_map/gather | solution.py:54
  43.6 7.5 %gather.22 = bf16[8,265,1536]{2,1,0:T(8,128)(2,1)} reshape(bf16[2120,1536]{1,0:T(8,128)(2,1)} %gather_fusion.1) | data formatting | bytes 13025280 | tf_op jit(solution)/shard_map/gather | solution.py:54
  51.2 0.2 broadcast_select_fusion.1
  51.4 6.2 %broadcast_select_fusion = bf16[8,265,1536]{2,1,0:T(8,128)(2,1)} fusion(bf16[8,265,1536]{2,1,0:T(8,128)(2,1)} %gather.22, pred[8,265]{1,0:T(8,128)(4,1)S(1)} %broadcast_compare_fusion), kind=kLoop, calls=%fused_computation.33 | loop fusion | flops 3256320 | bytes 13027400 | tf_op jit(solution)/shard_map/jit(_where)/select_n | solution.py:54
  57.6 7.0 %pad_maximum_fusion = bf16[8,329,1536]{2,1,0:T(8,128)(2,1)} fusion(bf16[8,64,1536]{2,1,0:T(8,128)(2,1)S(1)} %broadcast_select_fusion.1, bf16[8,265,1536]{2,1,0:T(8,128)(2,1)} %broadcast_select_fusion), kind=kLoop, calls=%fused_computation.23 | loop fusion | flops 16171008 | bytes 16171008 | tf_op jit(solution)/shard_map/concatenate | solution.py:57
  64.6 7.2 %all-to-all-start = ((bf16[8,329,1536]{2,1,0:T(8,128)(2,1)}), bf16[8,329,1536]{2,1,0:T(8,128)(2,1)}, u32[]{:S(2)}, u32[]{:S(2)}) async-start(bf16[8,329,1536]{2,1,0:T(8,128)(2,1)} %pad_maximum_fusion), calls=%async_computation | async-start | bytes 16515072 | tf_op jit(solution)/shard_map/all_to_all | solution.py:58
  71.8 92.1 %all-to-all-done = bf16[8,329,1536]{2,1,0:T(8,128)(2,1)} async-done(((bf16[8,329,1536]{2,1,0:T(8,128)(2,1)}), bf16[8,329,1536]{2,1,0:T(8,128)(2,1)}, u32[]{:S(2)}, u32[]{:S(2)}) %all-to-all-start) | async-done | bytes 8085536 | tf_op jit(solution)/shard_map/all_to_all | solution.py:58
  163.9 3.3 slice.75
  167.2 6.3 %copy.21 = bf16[8,265,1536]{2,0,1:T(8,128)(2,1)} copy(bf16[8,265,1536]{2,1,0:T(8,128)(2,1)S(1)} %slice.75) | data formatting | bytes 13025280 | tf_op jit(solution)/shard_map/slice | solution.py:59
  173.5 11.0 %fusion.28 = f32[5,8,53,512]{3,2,1,0:T(8,128)} fusion(bf16[5,1536,512]{2,1,0:T(8,128)(2,1)} %param.16, bf16[8,5,53,1536]{3,0,2,1:T(8,128)(2,1)} %bitcast.126), kind=kOutput, calls=%fused_computation.27 | convolution fusion | flops 3334471680 | bytes 18718720 | tf_op jit(solution)/shard_map/slcd,ldf->slcf/dot_general | solution.py:61
  184.5 18.8 %convert_bitcast_fusion = bf16[8,5,53,1536]{3,2,0,1:T(8,128)(2,1)} fusion(bf16[5,512,1536]{2,1,0:T(8,128)(2,1)} %param.17, f32[5,8,53,512]{3,2,1,0:T(8,128)} %fusion.28, bf16[5,1536,512]{2,1,0:T(8,128)(2,1)} %param.15, bf16[8,5,53,1536]{3,0,2,1:T(8,128)(2,1)} %bitcast.127), kind=kOutput, calls=%fused_computation.31 | convolution fusion | flops 6678712320 | bytes 33095680 | tf_op jit(solution)/shard_map/slcf,lfd->slcd/dot_general | solution.py:63
  203.3 5.2 %copy.24 = bf16[8,5,53,1536]{3,0,2,1:T(8,128)(2,1)S(1)} copy(bf16[8,5,53,1536]{3,2,0,1:T(8,128)(2,1)} %convert_bitcast_fusion) | data formatting | bytes 13025280 | tf_op jit(solution)/shard_map/convert_element_type | solution.py:63
  208.5 5.0 %copy.25 = bf16[8,265,1536]{2,1,0:T(8,128)(2,1)} copy(bf16[8,265,1536]{2,0,1:T(8,128)(2,1)S(1)} %bitcast.125) | data formatting | bytes 13025280 | tf_op jit(solution)/shard_map/reshape | solution.py:67
  213.5 0.4 conditional.1
  213.5 0.1 broadcast.186
  213.9 7.0 %pad_maximum_fusion.1 = bf16[8,329,1536]{2,1,0:T(8,128)(2,1)} fusion(bf16[8,64,1536]{2,1,0:T(8,128)(2,1)S(1)} %get-tuple-element.98, bf16[8,265,1536]{2,1,0:T(8,128)(2,1)} %copy.25), kind=kLoop, calls=%fused_computation.24 | loop fusion | flops 16171008 | bytes 16171008 | tf_op jit(solution)/shard_map/concatenate | solution.py:67
  220.9 0.0 copy-start.2
  220.9 14.5 %all-to-all-start.1 = ((bf16[8,329,1536]{2,1,0:T(8,128)(2,1)}), bf16[8,329,1536]{2,1,0:T(8,128)(2,1)}, u32[]{:S(2)}, u32[]{:S(2)}) async-start(bf16[8,329,1536]{2,1,0:T(8,128)(2,1)} %pad_maximum_fusion.1), calls=%async_computation.1 | async-start | bytes 16515072 | tf_op jit(solution)/shard_map/all_to_all | solution.py:68
  235.4 0.8 scatter_custom_fusion.3
  236.2 0.9 scatter_custom_fusion
  237.1 0.0 copy-done.2
  237.1 0.1 copy.31
  237.3 8.0 %scatter_custom_fusion.2 = s32[2048]{0:T(1024)S(1)} fusion(s32[2048]{0:T(1024)S(1)} %compare_select_fusion.10, s32[2048]{0:T(1024)S(1)} %iota.28, s32[]{:T(128)} %constant.21.clone.1), kind=kCustom, calls=%fused_computation.105 | custom fusion | bytes 8196 | tf_op jit(solution)/shard_map/scatter | solution.py:16
  245.4 0.6 fusion.63
  245.9 0.7 fusion.61
  246.7 0.7 fusion.62
  247.4 4.4 %compare_select_fusion.4 = (s32[2048,1]{0,1:T(1,128)S(1)}, s32[2048,1]{0,1:T(1,128)S(1)}) fusion(s32[]{:T(128)} %bitcast.55, s32[]{:T(128)} %bitcast.56, s32[]{:T(128)} %bitcast.57, s32[]{:T(128)} %bitcast.58, s32[]{:T(128)} %bitcast.59, s32[]{:T(128)} %bitcast.61, s32[]{:T(128)} %bitcast.60, s32[2048,1]{0,1:T(1,128)S(1)} %reshape.297), kind=kLoop, calls=%fused_computation.84 | loop fusion | flops 30720 | bytes 24604 | tf_op jit(solution)/shard_map/gather | solution.py:17
  251.8 0.8 compare_reduce_fusion.32
  252.6 20.7 %select_subtract_fusion = s32[2048]{0:T(1024)S(1)} fusion(pred[2048]{0:T(1024)(128)(4,1)S(1)} %get-tuple-element.55, pred[2048]{0:T(1024)(128)(4,1)S(1)} %get-tuple-element.54, pred[2048]{0:T(1024)(128)(4,1)S(1)} %get-tuple-element.53, pred[2048]{0:T(1024)(128)(4,1)S(1)} %get-tuple-element.52, pred[2048]{0:T(1024)(128)(4,1)S(1)} %get-tuple-element.51, ...), kind=kLoop, calls=%fused_computation.102 | loop fusion | flops 73728 | bytes 100484 | tf_op jit(solution)/shard_map/sub | solution.py:17
  273.3 0.1 concatenate.42
  273.4 0.1 copy.26
  273.5 0.1 copy.27
  273.6 0.2 reshape.377
  273.9 53.8 %all-to-all-done.1 = bf16[8,329,1536]{2,1,0:T(8,128)(2,1)} async-done(((bf16[8,329,1536]{2,1,0:T(8,128)(2,1)}), bf16[8,329,1536]{2,1,0:T(8,128)(2,1)}, u32[]{:S(2)}, u32[]{:S(2)}) %all-to-all-start.1) | async-done | bytes 8085536 | tf_op jit(solution)/shard_map/all_to_all | solution.py:68
  327.6 6.1 %slice.76 = bf16[8,265,1536]{2,1,0:T(8,128)(2,1)} slice(bf16[8,329,1536]{2,1,0:T(8,128)(2,1)} %all-to-all-done.1), slice={[0:8], [0:265], [0:1536]} | slice | bytes 13025280 | tf_op jit(solution)/shard_map/slice | solution.py:69
  333.8 7.5 %reshape.303 = bf16[2120,1536]{1,0:T(8,128)(2,1)} reshape(bf16[8,265,1536]{2,1,0:T(8,128)(2,1)} %slice.76) | data formatting | bytes 13025280 | tf_op jit(solution)/shard_map/reshape | solution.py:69
  341.2 1.0 slice_bitcast_fusion
  342.2 6.1 %pad_maximum_fusion.2 = bf16[2184,1536]{1,0:T(8,128)(2,1)} fusion(bf16[64,1536]{1,0:T(8,128)(2,1)S(1)} %slice_bitcast_fusion, bf16[2120,1536]{1,0:T(8,128)(2,1)} %reshape.303), kind=kLoop, calls=%fused_computation.32 | loop fusion | flops 13418496 | bytes 13418496 | tf_op jit(solution)/shard_map/concatenate | solution.py:69
  348.3 18.7 %gather_fusion.3 = bf16[2304,1536]{1,0:T(8,128)(2,1)} fusion(bf16[2184,1536]{1,0:T(8,128)(2,1)} %pad_maximum_fusion.2, s32[3072]{0:T(1024)S(1)} %pad_clamp_fusion), kind=kCustom, calls=%fused_computation.3 | custom fusion | bytes 14164992 | tf_op jit(solution)/shard_map/gather | solution.py:36
  366.9 13.3 %reshape.376 = bf16[256,9,1536]{2,1,0:T(8,128)(2,1)} reshape(bf16[2304,1536]{1,0:T(8,128)(2,1)} %gather_fusion.3) | data formatting | bytes 14155776 | tf_op jit(solution)/shard_map/gather | solution.py:36
  380.3 6.4 %fusion.64 = bf16[256,1,1536]{2,1,0:T(2,128)(2,1)S(1)} fusion(bf16[256,9,1]{1,2,0:T(2,128)(2,1)S(1)} %copy.31, bf16[256,9,1536]{2,1,0:T(8,128)(2,1)} %reshape.376), kind=kOutput, calls=%fused_computation.121 | convolution fusion | flops 7077888 | bytes 7868928 | tf_op jit(solution)/shard_map/tk,tkd->td/dot_general | solution.py:37
  386.7 1.0 copy.42
  387.7 0.0 copy-done.1
  (19 shorter events, 0.1 us)
Async XLA Ops:
  0.0 34.3 %copy-start = (bf16[256,1536]{1,0:T(8,128)(2,1)S(1)}, bf16[256,1536]{1,0:T(8,128)(2,1)}, u32[]{:S(2)}) copy-start(bf16[256,1536]{1,0:T(8,128)(2,1)} %param.10) | copy-start | bytes 2359300
  64.6 99.3 %all-to-all-start = ((bf16[8,329,1536]{2,1,0:T(8,128)(2,1)}), bf16[8,329,1536]{2,1,0:T(8,128)(2,1)}, u32[]{:S(2)}, u32[]{:S(2)}) async-start(bf16[8,329,1536]{2,1,0:T(8,128)(2,1)} %pad_maximum_fusion), calls=%async_computation | async-start | bytes 16515072 | tf_op jit(solution)/shard_map/all_to_all | solution.py:58
  220.9 16.2 %copy-start.2 = (f32[256,8]{0,1:T(8,128)S(1)}, f32[256,8]{0,1:T(8,128)}, u32[]{:S(2)}) copy-start(f32[256,8]{0,1:T(8,128)} %param.12) | copy-start | bytes 24580
  220.9 106.7 %all-to-all-start.1 = ((bf16[8,329,1536]{2,1,0:T(8,128)(2,1)}), bf16[8,329,1536]{2,1,0:T(8,128)(2,1)}, u32[]{:S(2)}, u32[]{:S(2)}) async-start(bf16[8,329,1536]{2,1,0:T(8,128)(2,1)} %pad_maximum_fusion.1), calls=%async_computation.1 | async-start | bytes 16515072 | tf_op jit(solution)/shard_map/all_to_all | solution.py:68
  380.3 7.4 %copy-start.1 = (bf16[256,1536]{1,0:T(8,128)(2,1)S(1)}, bf16[256,1536]{1,0:T(8,128)(2,1)}, u32[]{:S(2)}) copy-start(bf16[256,1536]{1,0:T(8,128)(2,1)} %param.10) | copy-start | bytes 2359300
where the time goes:
time: 395 us; the launch traced here: 388 us
  waiting for transfers between devices  146 us (37%)
  local copies, waits for them, and re-layouts  110 us (28%)
  other arithmetic  73.1 us (19%)
  matrix products  36.2 us (9%)
  starting transfers between devices  21.7 us (5%)
    all_to_all x1, waiting for transfers between devices, local_layer(): recv_buf = lax.all_to_all(send_buf, 'ep', 0, 0, tiled=True)  92.1 us
    all_to_all x1, waiting for transfers between devices, local_layer(): ret_buf = lax.all_to_all(back_buf, 'ep', 0, 0, tiled=True)  53.8 us
    gather x2, local copies, waits for them, and re-layouts, combine_rows(): picked = out_rows[all_slots]  32 us
    sub x1, other arithmetic, route_plan(): route_slot = flat_ids * cold_cap + route_rank - exp_starts[flat_ids]  20.7 us
    dot_general x1, matrix products, local_layer(): jnp.einsum('slcf,lfd->slcd', hidden, wd_loc, preferred_element_type=jnp.f...  18.8 us
    gather x2, local copies, waits for them, and re-layouts, local_layer(): cold_buf = jnp.where(filled[:, :, None], x_loc[src_route // top_k], 0)  16.1 us
    scatter-add x1, other arithmetic, route_plan(): exp_counts = jnp.bincount(flat_ids, length=num_experts).astype(jnp.int32)  14.7 us
    all_to_all x1, starting transfers between devices, local_layer(): ret_buf = lax.all_to_all(back_buf, 'ep', 0, 0, tiled=True)  14.5 us
  transfers between devices with their start and end apart: 2, of which 2 were waited for; matrix products, arithmetic and copies ran while one was open for 10% of the time, Pallas kernels for 0%

commit v1 on v0

v1 whole, which is shorter than its diff:
```python
import jax
import jax.numpy as jnp
from jax import lax
from jax.sharding import PartitionSpec as P


def gate_table(ids_loc, gates_loc, hot_loc, hot_g_loc, num_experts):
    num_tokens = ids_loc.shape[0]
    expert = jnp.arange(num_experts, dtype=jnp.int32)
    cold = jnp.sum(jnp.where(ids_loc[:, :, None] == expert, gates_loc[:, :, None], 0.0), axis=1)
    token = jnp.arange(num_tokens, dtype=jnp.int32)
    hot = jnp.sum(jnp.where(hot_loc[None, :] == token[:, None], hot_g_loc[None, :], 0.0), axis=1)
    return jnp.where(expert[None, :] == 0, hot[:, None], cold)


def solution(mesh):
    group_size = mesh.shape['ep']
    row_spec = P(('dp', 'ep'), None)
    list_spec = P(('dp', 'ep'))
    expert_spec = P('ep', None, None)

    def local_layer(x_loc, ids_loc, gates_loc, hot_loc, hot_g_loc, wg_loc, wu_loc, wd_loc):
        local_experts = wg_loc.shape[0]
        num_experts = local_experts * group_size
        table = gate_table(ids_loc, gates_loc, hot_loc, hot_g_loc, num_experts)
        x_all = lax.all_gather(x_loc, 'ep', axis=0, tiled=True)
        table = table.reshape(-1, group_size, local_experts)
        mine = lax.all_to_all(table, 'ep', 1, 0, tiled=True).reshape(-1, local_experts)
        total = jnp.zeros(x_all.shape, jnp.float32)
        for e in range(local_experts):
            gate_act = jnp.dot(x_all, wg_loc[e], preferred_element_type=jnp.float32)
            up_act = jnp.dot(x_all, wu_loc[e], preferred_element_type=jnp.float32)
            hidden = (jax.nn.silu(gate_act) * up_act).astype(jnp.bfloat16)
            out = jnp.dot(hidden, wd_loc[e], preferred_element_type=jnp.float32).astype(jnp.bfloat16)
            weight = mine[:, e:e + 1]
            total = total + jnp.where(weight != 0, weight * out.astype(jnp.float32), 0.0)
        return lax.psum_scatter(total, 'ep', scatter_dimension=0, tiled=True).astype(jnp.bfloat16)

    return jax.shard_map(local_layer, mesh=mesh,
                         in_specs=(row_spec, row_spec, row_spec, list_spec, list_spec, expert_spec, expert_spec, expert_spec),
                         out_specs=row_spec, check_vma=False)
```

time: 395 us -> 232 us (0.59); the launches traced: 388 us -> 232 us
  local copies, waits for them, and re-layouts: 110 us -> 0.05 us
  other arithmetic: 73.1 us -> 4.12 us
  matrix products: 36.2 us -> 103 us
  waiting for transfers between devices: 146 us -> 101 us
  starting transfers between devices: 21.7 us -> 0.06 us
  between operations: 0.71 us -> 13.5 us
  blocking collectives: 0 us -> 10.7 us
    all_to_all x2 -> x0, waiting for transfers between devices: 146 us -> none  [the longest x1 92.1 us: local_layer(): recv_buf = lax.all_to_all(send_buf, 'ep', 0, 0, tiled=True)]
    reduce_scatter x0 -> x1, waiting for transfers between devices: none -> 68.8 us  [local_layer(): lax.psum_scatter(total, 'ep', scatter_dimension=0, tiled=True)]
    dot_general x3 -> x10, matrix products: 36.2 us -> 103 us  [the longest x5 72 us: local_layer(): jnp.dot(hidden, wd_loc[e], preferred_element_type=jnp.float32)]
    gather x10 -> x0, local copies, waits for them, and re-layouts: 62.6 us -> none  [the longest x2 32 us: combine_rows(): picked = out_rows[all_slots]]
    all_gather x0 -> x1, waiting for transfers between devices: none -> 31.2 us  [local_layer(): x_all = lax.all_gather(x_loc, 'ep', axis=0, tiled=True)]
    all_to_all x2 -> x0, starting transfers between devices: 21.7 us -> none  [the longest x1 14.5 us: local_layer(): ret_buf = lax.all_to_all(back_buf, 'ep', 0, 0, tiled=True)]
    sub x2 -> x0, other arithmetic: 20.7 us -> none  [the longest x1 20.7 us: route_plan(): route_slot = flat_ids * cold_cap + route_rank - exp_starts[flat_ids]]
    concatenate x4 -> x0, other arithmetic: 20.1 us -> none  [the longest x1 7.03 us: local_layer(): jnp.concatenate([cold_out.reshape(group_size, block_rows, d_model), hot_o...]
  transfers between devices with their start and end apart: 2 -> 2, of which waited for: 2 -> 2; matrix products, arithmetic and copies ran while one was open for 10% -> 1% of each run, Pallas kernels for 0% -> 0%
where the time goes in v1:
time: 232 us
  matrix products  103 us (44%)
  waiting for transfers between devices  101 us (44%)
  between operations  13.5 us (6%)
  blocking collectives  10.7 us (5%)
  other arithmetic  4.12 us (2%)
    dot_general x5, matrix products, local_layer(): jnp.dot(hidden, wd_loc[e], preferred_element_type=jnp.float32)  72 us
    reduce_scatter x1, waiting for transfers between devices, local_layer(): lax.psum_scatter(total, 'ep', scatter_dimension=0, tiled=True)  68.8 us
    all_gather x1, waiting for transfers between devices, local_layer(): x_all = lax.all_gather(x_loc, 'ep', axis=0, tiled=True)  31.2 us
    dot_general x5, matrix products, local_layer(): gate_act = jnp.dot(x_all, wg_loc[e], preferred_element_type=jnp.float32)  31 us
    all_to_all x1, blocking collectives, local_layer(): lax.all_to_all(table, 'ep', 1, 0, tiled=True).reshape(-1, local_experts)  10.7 us
  transfers between devices with their start and end apart: 2, of which 2 were waited for; matrix products, arithmetic and copies ran while one was open for 1% of the time, Pallas kernels for 0%

profile of v1, /device:TPU:81, one launch (start us, length us, event | category | flops | bytes accessed | tf_op | source)
XLA Modules:
  0.0 232.1 jit_solution(4994321369470178643)
XLA Ops:
  6.5 0.0 all-gather.2.cloned.1.call-start
  6.6 0.7 all-gather.2.cloned.1.call-update
  7.3 0.1 reduce-scatter.2.cloned.1.call-start
  7.4 0.8 select_reduce_fusion
  8.2 0.8 select_reduce_fusion.1
  8.9 0.1 broadcast_select_fusion
  9.0 10.7 %all_to_all.15 = f32[256,8,5]{0,2,1:T(8,128)S(1)} all-to-all(f32[256,8,5]{0,2,1:T(8,128)S(1)} %broadcast_select_fusion), channel_id=1, replica_groups=mesh['dp'=4,'ep'=8] {'ep'}, dimensions={1} | all-to-all | bytes 81920 | tf_op jit(solution)/shard_map/all_to_all | solution.py:28
  19.7 0.1 compare_reduce_fusion.4
  19.8 31.2 %all-gather.2.cloned.1.call-done = bf16[2048,1536]{1,0:T(8,128)(2,1)} async-done(((bf16[256,1536]{1,0:T(8,128)(2,1)}), bf16[2048,1536]{1,0:T(8,128)(2,1)}) %all-gather.2.cloned.1.call-update) | async-done | bytes 6291472 | tf_op jit(solution)/shard_map/all_gather | solution.py:26
  51.0 0.0 copy-start
  51.0 0.0 slice-start
  51.0 8.8 %fusion.2 = f32[2048,512]{1,0:T(8,128)} fusion(bf16[2048,1536]{1,0:T(8,128)(2,1)} %all-gather.2.cloned.1.call-done, bf16[5,1536,512]{2,1,0:T(8,128)(2,1)} %param.13), kind=kOutput, calls=%fused_computation.13 | convolution fusion | flops 3221225472 | bytes 12058624 | tf_op jit(solution)/shard_map/dot_general | solution.py:31
  59.8 0.0 copy-done
  59.8 0.0 slice-start.1
  59.8 6.5 %fusion.6 = f32[2048,512]{1,0:T(8,128)} fusion(bf16[2048,1536]{1,0:T(8,128)(2,1)S(1)} %copy-done, bf16[5,1536,512]{2,1,0:T(8,128)(2,1)} %param.13), kind=kOutput, calls=%fused_computation.17 | convolution fusion | flops 3221225472 | bytes 12058624 | tf_op jit(solution)/shard_map/dot_general | solution.py:31
  66.3 0.0 slice-done
  66.3 0.0 slice-done.1
  66.3 5.3 %fusion.10 = f32[2048,512]{1,0:T(8,128)} fusion(bf16[2048,1536]{1,0:T(8,128)(2,1)S(1)} %copy-done, bf16[5,1536,512]{2,1,0:T(8,128)(2,1)S(1)} %bitcast.85), kind=kOutput, calls=%fused_computation.21 | convolution fusion | flops 3221225472 | bytes 12058624 | tf_op jit(solution)/shard_map/dot_general | solution.py:31
  71.5 5.2 %fusion.14 = f32[2048,512]{1,0:T(8,128)} fusion(bf16[2048,1536]{1,0:T(8,128)(2,1)S(1)} %copy-done, bf16[5,1536,512]{2,1,0:T(8,128)(2,1)S(1)} %bitcast.85), kind=kOutput, calls=%fused_computation.25 | convolution fusion | flops 3221225472 | bytes 12058624 | tf_op jit(solution)/shard_map/dot_general | solution.py:31
  76.8 5.2 %fusion.18 = f32[2048,512]{1,0:T(8,128)} fusion(bf16[2048,1536]{1,0:T(8,128)(2,1)S(1)} %copy-done, bf16[5,1536,512]{2,1,0:T(8,128)(2,1)S(1)} %bitcast.85), kind=kOutput, calls=%fused_computation.29 | convolution fusion | flops 3221225472 | bytes 12058624 | tf_op jit(solution)/shard_map/dot_general | solution.py:31
  82.0 12.1 %convolution_convert_fusion = bf16[2048,1536]{1,0:T(8,128)(2,1)} fusion(bf16[5,512,1536]{2,1,0:T(8,128)(2,1)} %param.15, f32[2048,512]{1,0:T(8,128)} %fusion.2, bf16[2048,1536]{1,0:T(8,128)(2,1)} %all-gather.2.cloned.1.call-done, bf16[5,1536,512]{2,1,0:T(8,128)(2,1)} %param.14), kind=kOutput, calls=%fused_computation.1 | convolution fusion | flops 6451888128 | bytes 19922944 | tf_op jit(solution)/shard_map/dot_general | solution.py:34
  94.1 12.4 %convolution_convert_fusion.1 = bf16[2048,1536]{1,0:T(8,128)(2,1)} fusion(bf16[5,512,1536]{2,1,0:T(8,128)(2,1)} %param.15, f32[2048,512]{1,0:T(8,128)} %fusion.6, bf16[2048,1536]{1,0:T(8,128)(2,1)} %all-gather.2.cloned.1.call-done, bf16[5,1536,512]{2,1,0:T(8,128)(2,1)} %param.14), kind=kOutput, calls=%fused_computation.2 | convolution fusion | flops 6451888128 | bytes 19922944 | tf_op jit(solution)/shard_map/dot_general | solution.py:34
  106.5 12.2 %convolution_convert_fusion.2 = bf16[2048,1536]{1,0:T(8,128)(2,1)} fusion(bf16[5,512,1536]{2,1,0:T(8,128)(2,1)} %param.15, f32[2048,512]{1,0:T(8,128)} %fusion.10, bf16[2048,1536]{1,0:T(8,128)(2,1)} %all-gather.2.cloned.1.call-done, bf16[5,1536,512]{2,1,0:T(8,128)(2,1)} %param.14), kind=kOutput, calls=%fused_computation.3 | convolution fusion | flops 6451888128 | bytes 19922944 | tf_op jit(solution)/shard_map/dot_general | solution.py:34
  118.6 12.1 %convolution_convert_fusion.3 = bf16[2048,1536]{1,0:T(8,128)(2,1)} fusion(bf16[5,512,1536]{2,1,0:T(8,128)(2,1)} %param.15, f32[2048,512]{1,0:T(8,128)} %fusion.14, bf16[2048,1536]{1,0:T(8,128)(2,1)} %all-gather.2.cloned.1.call-done, bf16[5,1536,512]{2,1,0:T(8,128)(2,1)} %param.14), kind=kOutput, calls=%fused_computation.4 | convolution fusion | flops 6451888128 | bytes 19922944 | tf_op jit(solution)/shard_map/dot_general | solution.py:34
  130.7 23.3 %select_add_fusion = f32[2048,1536]{1,0:T(8,128)} fusion(bf16[2048,1536]{1,0:T(8,128)(2,1)} %convolution_convert_fusion, bf16[2048,1536]{1,0:T(8,128)(2,1)} %convolution_convert_fusion.1, bf16[2048,1536]{1,0:T(8,128)(2,1)} %convolution_convert_fusion.2, bf16[2048,1536]{1,0:T(8,128)(2,1)} %convolution_convert_fusion.3, f32[2048]{0:T(1024)S(1)} %bitcast.80, ...), kind=kOutput, calls=%fused_computation | convolution fusion | flops 6511656960 | bytes 51431424 | tf_op jit(solution)/shard_map/dot_general | solution.py:34
  154.0 0.1 reduce-scatter.2.cloned.1.call-update
  154.1 68.8 %reduce-scatter.2.cloned.1.call-done = f32[256,1536]{1,0:T(8,128)} async-done(((f32[2048,1536]{1,0:T(8,128)}), f32[256,1536]{1,0:T(8,128)}) %reduce-scatter.2.cloned.1.call-update) | async-done | bytes 1572880 | tf_op jit(solution)/shard_map/reduce_scatter | solution.py:37
  222.9 2.4 %convert_element_type.63 = bf16[256,1536]{1,0:T(8,128)(2,1)} convert(f32[256,1536]{1,0:T(8,128)} %reduce-scatter.2.cloned.1.call-done) | non-fusion elementwise | flops 393216 | bytes 2359296 | tf_op jit(solution)/shard_map/convert_element_type | solution.py:37
  (4 shorter events, 0.0 us)
Async XLA Ops:
  6.5 44.5 %all-gather.2.cloned.1.call-start = ((), (), s32[]{:S(2)}) async-start(), calls=%async_computation.2 | async-start | bytes 7077888 | tf_op jit(solution)/shard_map/all_gather | solution.py:26
  7.3 215.6 %reduce-scatter.2.cloned.1.call-start = ((), (), s32[]{:S(2)}) async-start(), calls=%async_computation.3 | async-start | bytes 14155776 | tf_op jit(solution)/shard_map/reduce_scatter | solution.py:37
  51.0 8.8 %copy-start = (bf16[2048,1536]{1,0:T(8,128)(2,1)S(1)}, bf16[2048,1536]{1,0:T(8,128)(2,1)}, u32[]{:S(2)}) copy-start(bf16[2048,1536]{1,0:T(8,128)(2,1)} %all-gather.2.cloned.1.call-done) | copy-start | bytes 18874372
  51.0 15.3 %slice-start = ((s8[7864320]{0:T(1024)(128)(4,1)}), s8[4194304]{0:T(1024)(128)(4,1)S(1)}, s32[]{:S(2)}) async-start(s8[7864320]{0:T(1024)(128)(4,1)} %bitcast.84), calls=%async_computation.4 | async-start | bytes 8388608
  59.8 6.5 %slice-start.1 = ((s8[7864320]{0:T(1024)(128)(4,1)}), s8[3670016]{0:T(1024)(128)(4,1)S(1)}, s32[]{:S(2)}) async-start(s8[7864320]{0:T(1024)(128)(4,1)} %bitcast.84), calls=%async_computation.5 | async-start | bytes 7340032
Sparse Core Ops, SparseCore 0:
  8.9 42.0 all-gather.1
  154.2 68.6 reduce-scatter.1

commit v2 on v1

v2 whole, which is shorter than its diff:
```python
import functools

import jax
import jax.numpy as jnp
from jax import lax
from jax.experimental import pallas as pl
from jax.experimental.pallas import tpu as pltpu
from jax.sharding import PartitionSpec as P

CHIPS = 4
QUARTERS = 4
LANES = 8


def gate_table(ids_loc, gates_loc, hot_loc, hot_g_loc, group_size, local_experts):
    num_tokens = ids_loc.shape[0]
    slot = jnp.arange(group_size * LANES, dtype=jnp.int32)
    local = slot % LANES
    expert = jnp.where(local < local_experts, (slot // LANES) * local_experts + local, -1)
    token = jnp.arange(num_tokens, dtype=jnp.int32)
    cold = jnp.sum(jnp.where(ids_loc.T[:, None, :] == expert[None, :, None], gates_loc.T[:, None, :], 0.0), axis=0)
    hot = jnp.sum(jnp.where(hot_loc[:, None] == token[None, :], hot_g_loc[:, None], 0.0), axis=0)
    table = jnp.where(expert[:, None] == 0, hot[None, :], cold)
    return table.reshape(group_size, LANES, num_tokens)


def moe_kernel(x_hbm, tab_ref, wg_hbm, wu_hbm, wd_hbm, out_hbm,
               xall, wg, wu, wd, part, mate, ring, from_right, from_left, tabs, gcol, stage,
               w_sem, x_sem, ag_send, ag_recv, md_send, md_recv, tb_send, tb_recv,
               pd_send, pd_recv, rs_send, rs_recv, out_sem):
    experts = wg.shape[0]
    rows = xall.shape[2] // QUARTERS
    me = lax.axis_index('ep')
    chip, core = me // 2, me % 2
    right = ((chip + 1) % CHIPS) * 2 + core
    left = ((chip + CHIPS - 1) % CHIPS) * 2 + core
    partner = chip * 2 + (1 - core)

    def piece(p):
        return pl.ds(p * rows, rows)

    def remote(src, dst, send, recv, device):
        return pltpu.make_async_remote_copy(src_ref=src, dst_ref=dst, send_sem=send, recv_sem=recv,
                                            device_id={'ep': device}, device_id_type=pl.DeviceIdType.MESH)

    sends = []

    def start(make):
        make().start()
        sends.append(make)

    x_copy = pltpu.make_async_copy(x_hbm, xall.at[0, 0], x_sem)
    x_copy.start()
    w_copies = []
    for e in range(experts):
        for i, (src, dst) in enumerate(((wg_hbm, wg), (wu_hbm, wu), (wd_hbm, wd))):
            w_copies.append(pltpu.make_async_copy(src.at[e], dst.at[e], w_sem.at[3 * e + i]))
    for copy in w_copies:
        copy.start()

    barrier = pltpu.get_barrier_semaphore()
    peers = [(((chip + o) % CHIPS) * 2 + (core + q) % 2, o, q) for o in range(CHIPS) for q in range(2) if o or q]
    for device, _, _ in peers:
        pl.semaphore_signal(barrier, inc=1, device_id={'ep': device}, device_id_type=pl.DeviceIdType.MESH)
    pl.semaphore_wait(barrier, len(peers))

    def ring_send(o_src, o_dst, p, device):
        start(lambda: remote(xall.at[o_src, 0, piece(p)], xall.at[o_dst, 0, piece(p)],
                             ag_send.at[o_dst, p], ag_recv.at[o_dst, p], device))

    def mate_send(o, p):
        start(lambda: remote(xall.at[o, 0, piece(p)], xall.at[o, 1, piece(p)],
                             md_send.at[o, p], md_recv.at[o, p], partner))

    def ring_arrived(o, p):
        remote(xall.at[o, 0, piece(p)], xall.at[o, 0, piece(p)],
               ag_send.at[o, p], ag_recv.at[o, p], right).wait_recv()
        mate_send(o, p)

    def mate_arrived(o, p):
        remote(xall.at[o, 1, piece(p)], xall.at[o, 1, piece(p)],
               md_send.at[o, p], md_recv.at[o, p], partner).wait_recv()

    x_copy.wait()
    for p in (0, 1):
        ring_send(0, 3, p, right)
        ring_send(0, 1, p + 2, left)
    for p in range(QUARTERS):
        mate_send(0, p)
    for device, o, q in peers:
        start(functools.partial(remote, tab_ref.at[device], tabs.at[(CHIPS - o) % CHIPS, q], tb_send.at[o, q],
                                tb_recv.at[(CHIPS - o) % CHIPS, q], device))
    tabs[0, 0] = tab_ref[me]

    lane = lax.broadcasted_iota(jnp.int32, (rows, LANES), 1)

    def gates_ready(o, q):
        if o or q:
            remote(tabs.at[o, q], tabs.at[o, q], tb_send.at[o, q], tb_recv.at[o, q], partner).wait_recv()
        gcol[o, q] = jnp.transpose(tabs[o, q])

    def run_chunk(pairs, hooks, wait_weights):
        groups = [(o, q, p) for o, p in pairs for q in range(2)]
        for o, q, p in groups:
            part[o, q, piece(p)] = jnp.zeros((rows, part.shape[3]), jnp.float32)

        def body(e, _):
            for step, hook in hooks:
                pl.when(e == step)(hook)
            if wait_weights:
                for i in range(3):
                    ref = (wg, wu, wd)[i]
                    pltpu.make_async_copy(ref.at[e], ref.at[e], w_sem.at[3 * e + i]).wait()
            x = jnp.concatenate([xall[o, q, piece(p)] for o, q, p in groups], axis=0)
            half = wg.shape[2] // 2
            hidden = []
            for n in range(2):
                cols = pl.ds(n * half, half)
                a = jnp.dot(x, wg[e, :, cols], preferred_element_type=jnp.float32)
                b = jnp.dot(x, wu[e, :, cols], preferred_element_type=jnp.float32)
                hidden.append((a * jax.nn.sigmoid(a) * b).astype(jnp.bfloat16))
            u = jnp.concatenate(hidden, axis=1)
            weight = [jnp.sum(jnp.where(lane == e, gcol[o, q, piece(p)], 0.0), axis=1, keepdims=True)
                      for o, q, p in groups]
            width = 512
            for n in range(wd.shape[2] // width):
                cols = pl.ds(n * width, width)
                h = jnp.dot(u, wd[e, :, cols], preferred_element_type=jnp.float32).astype(jnp.bfloat16).astype(jnp.float32)
                for i, (o, q, p) in enumerate(groups):
                    hi = h[i * rows:(i + 1) * rows]
                    part[o, q, piece(p), cols] += jnp.where(weight[i] != 0, weight[i] * hi, 0.0)
            return 0

        lax.fori_loop(0, experts, body, 0)
        for o, p in pairs:
            start(functools.partial(remote, part.at[o, 1, piece(p)], mate.at[o, piece(p)],
                                    pd_send.at[o, p], pd_recv.at[o, p], partner))

    def partner_sum(o, p):
        remote(mate.at[o, piece(p)], mate.at[o, piece(p)], pd_send.at[o, p], pd_recv.at[o, p], partner).wait_recv()
        return part[o, 0, piece(p)] + mate[o, piece(p)]

    def rs_transfer(o, p, device):
        dst = {2: ring, 3: from_right, 1: from_left}[o]
        return remote(part.at[o, 0, piece(p)], dst.at[piece(p)], rs_send.at[o, p], rs_recv.at[o, p], device)

    def finish(o, p):
        total = partner_sum(o, p)
        goes_left = o == 3 or (o == 2 and p < 2)
        if (o == 3 and p < 2) or (o == 1 and p >= 2):
            rs_transfer(2, p, left).wait_recv()
            total = total + ring[piece(p)]
        part[o, 0, piece(p)] = total
        start(functools.partial(rs_transfer, o, p, left if goes_left else right))

    def forward(i):
        ring_arrived(3, i)
        ring_send(3, 2, i, right)
        ring_arrived(1, i + 2)
        ring_send(1, 2, i + 2, left)

    def forward_last():
        forward(1)
        for p in (0, 1):
            ring_send(0, 3, p + 2, right)
            ring_send(0, 1, p, left)

    def far(i):
        ring_arrived(2, i)
        ring_arrived(2, i + 2)

    def near(i):
        ring_arrived(3, i + 2)
        ring_arrived(1, i)

    def both(o1, p1, o2, p2):
        def act():
            finish(o1, p1)
            finish(o2, p2)
        return act

    def mates(*items):
        for o, p in items:
            mate_arrived(o, p)

    gates_ready(0, 0)
    gates_ready(0, 1)
    mates(*[(0, p) for p in range(QUARTERS)])
    run_chunk([(0, 0), (0, 2)], [(4, lambda: forward(0))], True)
    run_chunk([(0, 1), (0, 3)], [(2, forward_last), (4, lambda: far(0))], False)
    gates_ready(2, 0)
    gates_ready(2, 1)
    mates((2, 0), (2, 2))
    run_chunk([(2, 0), (2, 2)], [(3, lambda: far(1))], False)
    mates((2, 1), (2, 3))
    run_chunk([(2, 1), (2, 3)], [(1, both(2, 0, 2, 2)), (3, lambda: near(0))], False)
    for o in (1, 3):
        for q in range(2):
            gates_ready(o, q)
    mates((3, 2), (1, 0))
    run_chunk([(3, 2), (1, 0)], [(1, both(2, 1, 2, 3)), (3, lambda: near(1))], False)
    mates((3, 3), (1, 1))
    run_chunk([(3, 3), (1, 1)], [(1, both(3, 2, 1, 0))], False)
    mates((3, 0), (1, 2))
    run_chunk([(3, 0), (1, 2)], [(1, both(3, 3, 1, 1))], False)
    mates((3, 1), (1, 3))
    run_chunk([(3, 1), (1, 3)], [(1, both(3, 0, 1, 2))], False)
    both(3, 1, 1, 3)()

    for p in range(QUARTERS):
        part[0, 0, piece(p)] = partner_sum(0, p)
    out_copies = []
    for p in (0, 2, 1, 3):
        rs_transfer(3, p, left).wait_recv()
        rs_transfer(1, p, left).wait_recv()
        total = part[0, 0, piece(p)] + from_right[piece(p)] + from_left[piece(p)]
        stage[piece(p)] = total.astype(stage.dtype)
        copy = pltpu.make_async_copy(stage.at[piece(p)], out_hbm.at[piece(p)], out_sem.at[p])
        copy.start()
        out_copies.append(copy)
    for make in sends:
        make().wait_send()
    for copy in out_copies:
        copy.wait()


def solution(mesh):
    group_size = mesh.shape['ep']
    row_spec = P(('dp', 'ep'), None)
    list_spec = P(('dp', 'ep'))
    expert_spec = P('ep', None, None)

    def local_layer(x_loc, ids_loc, gates_loc, hot_loc, hot_g_loc, wg_loc, wu_loc, wd_loc):
        experts, d_model, d_ff = wg_loc.shape
        tokens = x_loc.shape[0]
        table = gate_table(ids_loc, gates_loc, hot_loc, hot_g_loc, group_size, experts)
        any_spec = pl.BlockSpec(memory_space=pl.ANY)
        dma = pltpu.SemaphoreType.DMA
        f32, bf16 = jnp.float32, jnp.bfloat16
        return pl.pallas_call(
            moe_kernel,
            out_shape=jax.ShapeDtypeStruct(x_loc.shape, x_loc.dtype),
            in_specs=[any_spec, pl.BlockSpec(memory_space=pltpu.VMEM), any_spec, any_spec, any_spec],
            out_specs=any_spec,
            scratch_shapes=[
                pltpu.VMEM((CHIPS, 2, tokens, d_model), bf16),
                pltpu.VMEM((experts, d_model, d_ff), bf16),
                pltpu.VMEM((experts, d_model, d_ff), bf16),
                pltpu.VMEM((experts, d_ff, d_model), bf16),
                pltpu.VMEM((CHIPS, 2, tokens, d_model), f32),
                pltpu.VMEM((CHIPS, tokens, d_model), f32),
                pltpu.VMEM((tokens, d_model), f32),
                pltpu.VMEM((tokens, d_model), f32),
                pltpu.VMEM((tokens, d_model), f32),
                pltpu.VMEM((CHIPS, 2, LANES, tokens), f32),
                pltpu.VMEM((CHIPS, 2, tokens, LANES), f32),
                pltpu.VMEM((tokens, d_model), bf16),
                dma((3 * experts,)), dma,
                dma((CHIPS, QUARTERS)), dma((CHIPS, QUARTERS)),
                dma((CHIPS, QUARTERS)), dma((CHIPS, QUARTERS)),
                dma((CHIPS, 2)), dma((CHIPS, 2)),
                dma((CHIPS, QUARTERS)), dma((CHIPS, QUARTERS)),
                dma((CHIPS, QUARTERS)), dma((CHIPS, QUARTERS)),
                dma((QUARTERS,)),
            ],
            compiler_params=pltpu.CompilerParams(collective_id=0, has_side_effects=True, vmem_limit_bytes=67_043_328),
            cost_estimate=pl.CostEstimate(flops=100_000_000, bytes_accessed=30_000_000, transcendentals=0),
            name='moe_ring',
        )(x_loc, table, wg_loc, wu_loc, wd_loc)

    return jax.shard_map(local_layer, mesh=mesh,
                         in_specs=(row_spec, row_spec, row_spec, list_spec, list_spec, expert_spec, expert_spec, expert_spec),
                         out_specs=row_spec, check_vma=False)
```

time: 232 us -> 96.9 us (0.42)
  matrix products: 103 us -> 0 us
  waiting for transfers between devices: 101 us -> 0 us
  Pallas kernels: 0 us -> 92.2 us
  between operations: 13.5 us -> 0.02 us
  blocking collectives: 10.7 us -> 0 us
    dot_general x10 -> x0, matrix products: 103 us -> none  [the longest x5 72 us: local_layer(): jnp.dot(hidden, wd_loc[e], preferred_element_type=jnp.float32)]
    pallas_call x0 -> x1, Pallas kernels: none -> 92.2 us  [local_layer(): pl.pallas_call(moe_kernel, out_shape=jax.ShapeDtypeStruct(x_loc.shape, x_...]
    reduce_scatter x1 -> x0, waiting for transfers between devices: 68.8 us -> none  [local_layer(): lax.psum_scatter(total, 'ep', scatter_dimension=0, tiled=True)]
    all_gather x1 -> x0, waiting for transfers between devices: 31.2 us -> none  [local_layer(): x_all = lax.all_gather(x_loc, 'ep', axis=0, tiled=True)]
    all_to_all x1 -> x0, blocking collectives: 10.7 us -> none  [local_layer(): lax.all_to_all(table, 'ep', 1, 0, tiled=True).reshape(-1, local_experts)]
    convert_element_type x1 -> x0, other arithmetic: 2.37 us -> none  [local_layer(): lax.psum_scatter(total, 'ep', scatter_dimension=0, tiled=True)]
  transfers between devices with their start and end apart: 2 -> 0, of which waited for: 2 -> 0; matrix products, arithmetic and copies ran while one was open for 1% -> 0% of each run, Pallas kernels for 0% -> 0%
where the time goes in v2:
time: 96.9 us; the launch traced here: 96.7 us
  Pallas kernels  92.2 us (95%)
  other arithmetic  2.34 us (2%)
  local copies, waits for them, and re-layouts  2.06 us (2%)
    pallas_call x1, Pallas kernels, local_layer(): pl.pallas_call(moe_kernel, out_shape=jax.ShapeDtypeStruct(x_loc.shape, x_...  92.2 us
    unnamed x1, local copies, waits for them, and re-layouts  2.06 us

profile of v2, /device:TPU:81, one launch (start us, length us, event | category | flops | bytes accessed | tf_op | source)
XLA Modules:
  0.0 96.7 jit_solution(5022732645864630002)
XLA Ops:
  0.0 0.8 select_reduce_fusion.1
  0.8 0.8 select_reduce_fusion
  1.6 0.7 bitcast_select_fusion.tab_ref
  2.3 92.2 %moe_ring.1 = bf16[256,1536]{1,0:T(8,128)(2,1)} custom-call(bf16[256,1536]{1,0:T(8,128)(2,1)} %x_hbm.1, f32[8,8,256]{2,1,0:T(8,128)} %bitcast_select_fusion.tab_ref, bf16[5,1536,512]{2,1,0:T(8,128)(2,1)} %wg_hbm.1, bf16[5,1536,512]{2,1,0:T(8,128)(2,1)} %wu_hbm.1, bf16[5,512,1536]{2,1,0:T(8,128)(2,1)} %wd_hbm.1), custom_call_target="tpu_custom_call" | custom-call | flops 100000000 | bytes 30000000 | tf_op jit(solution)/shard_map/moe_ring/pallas_call | solution.py:240
  94.6 2.1 %copy.10 = bf16[256,1536]{1,0:T(8,128)(2,1)} copy(bf16[256,1536]{1,0:T(8,128)(2,1)} %moe_ring.1) | data formatting | bytes 1572864
  (2 shorter events, 0.0 us)

commit v3 on v2

--- a/solution.py
+++ b/solution.py
@@ -12,21 +12,27 @@
 LANES = 8
 
 
-def gate_table(ids_loc, gates_loc, hot_loc, hot_g_loc, group_size, local_experts):
-    num_tokens = ids_loc.shape[0]
-    slot = jnp.arange(group_size * LANES, dtype=jnp.int32)
-    local = slot % LANES
-    expert = jnp.where(local < local_experts, (slot // LANES) * local_experts + local, -1)
-    token = jnp.arange(num_tokens, dtype=jnp.int32)
-    cold = jnp.sum(jnp.where(ids_loc.T[:, None, :] == expert[None, :, None], gates_loc.T[:, None, :], 0.0), axis=0)
-    hot = jnp.sum(jnp.where(hot_loc[:, None] == token[None, :], hot_g_loc[:, None], 0.0), axis=0)
-    table = jnp.where(expert[:, None] == 0, hot[None, :], cold)
-    return table.reshape(group_size, LANES, num_tokens)
-
-
-def moe_kernel(x_hbm, tab_ref, wg_hbm, wu_hbm, wd_hbm, out_hbm,
-               xall, wg, wu, wd, part, mate, ring, from_right, from_left, tabs, gcol, stage,
-               w_sem, x_sem, ag_send, ag_recv, md_send, md_recv, tb_send, tb_recv,
+def build_table(ids, gates, hot_ref, hot_g_ref, tab_ref, experts):
+    devices, padded, tokens = tab_ref.shape
+    token_ids, token_gates = ids[...], gates[...]
+    slot = lax.broadcasted_iota(jnp.int32, (padded, tokens), 0)
+    token = lax.broadcasted_iota(jnp.int32, (1, tokens), 1)
+
+    def add_hot(r, row):
+        return jnp.where(token == hot_ref[r], hot_g_ref[r], row)
+
+    hot = lax.fori_loop(0, hot_ref.shape[0], add_hot, jnp.zeros((1, tokens), jnp.float32), unroll=8)
+    for d in range(devices):
+        expert = jnp.where(slot < experts, d * experts + slot, -1)
+        table = jnp.zeros((padded, tokens), jnp.float32)
+        for j in range(token_ids.shape[0]):
+            table = jnp.where(token_ids[j:j + 1] == expert, token_gates[j:j + 1], table)
+        tab_ref[d] = jnp.where(expert == 0, hot, table)
+
+
+def moe_kernel(hot_ref, hot_g_ref, x_hbm, ids_hbm, gates_hbm, wg_hbm, wu_hbm, wd_hbm, out_hbm,
+               ids, gates, tab_ref, xall, wg, wu, wd, part, mate, ring, from_right, from_left, tabs, gcol, stage,
+               w_sem, x_sem, in_sem, ag_send, ag_recv, md_send, md_recv, tb_send, tb_recv,
                pd_send, pd_recv, rs_send, rs_recv, out_sem):
     experts = wg.shape[0]
     rows = xall.shape[2] // QUARTERS
@@ -55,7 +61,8 @@
     for e in range(experts):
         for i, (src, dst) in enumerate(((wg_hbm, wg), (wu_hbm, wu), (wd_hbm, wd))):
             w_copies.append(pltpu.make_async_copy(src.at[e], dst.at[e], w_sem.at[3 * e + i]))
-    for copy in w_copies:
+    in_copies = [pltpu.make_async_copy(ids_hbm, ids, in_sem.at[0]), pltpu.make_async_copy(gates_hbm, gates, in_sem.at[1])]
+    for copy in in_copies:
         copy.start()
 
     barrier = pltpu.get_barrier_semaphore()
@@ -87,6 +94,11 @@
         ring_send(0, 1, p + 2, left)
     for p in range(QUARTERS):
         mate_send(0, p)
+    for copy in w_copies:
+        copy.start()
+    for copy in in_copies:
+        copy.wait()
+    build_table(ids, gates, hot_ref, hot_g_ref, tab_ref, experts)
     for device, o, q in peers:
         start(functools.partial(remote, tab_ref.at[device], tabs.at[(CHIPS - o) % CHIPS, q], tb_send.at[o, q],
                                 tb_recv.at[(CHIPS - o) % CHIPS, q], device))
@@ -99,15 +111,16 @@
             remote(tabs.at[o, q], tabs.at[o, q], tb_send.at[o, q], tb_recv.at[o, q], partner).wait_recv()
         gcol[o, q] = jnp.transpose(tabs[o, q])
 
-    def run_chunk(pairs, hooks, wait_weights):
+    def run_chunk(pairs, first, last, hooks):
         groups = [(o, q, p) for o, p in pairs for q in range(2)]
-        for o, q, p in groups:
-            part[o, q, piece(p)] = jnp.zeros((rows, part.shape[3]), jnp.float32)
+        if first == 0:
+            for o, q, p in groups:
+                part[o, q, piece(p)] = jnp.zeros((rows, part.shape[3]), jnp.float32)
 
         def body(e, _):
             for step, hook in hooks:
                 pl.when(e == step)(hook)
-            if wait_weights:
+            if (pairs, first) == ([(0, 0), (0, 2)], 0):
                 for i in range(3):
                     ref = (wg, wu, wd)[i]
                     pltpu.make_async_copy(ref.at[e], ref.at[e], w_sem.at[3 * e + i]).wait()
@@ -131,8 +144,8 @@
                     part[o, q, piece(p), cols] += jnp.where(weight[i] != 0, weight[i] * hi, 0.0)
             return 0
 
-        lax.fori_loop(0, experts, body, 0)
-        for o, p in pairs:
+        lax.fori_loop(first, last, body, 0)
+        for o, p in pairs if last == experts else ():
             start(functools.partial(remote, part.at[o, 1, piece(p)], mate.at[o, piece(p)],
                                     pd_send.at[o, p], pd_recv.at[o, p], partner))
 
@@ -186,26 +199,26 @@
     gates_ready(0, 0)
     gates_ready(0, 1)
     mates(*[(0, p) for p in range(QUARTERS)])
-    run_chunk([(0, 0), (0, 2)], [(4, lambda: forward(0))], True)
-    run_chunk([(0, 1), (0, 3)], [(2, forward_last), (4, lambda: far(0))], False)
-    gates_ready(2, 0)
-    gates_ready(2, 1)
+    run_chunk([(0, 0), (0, 2)], 0, experts, [(2, lambda: forward(0)), (4, forward_last)])
+    run_chunk([(0, 1), (0, 3)], 0, 3, [(2, lambda: far(0))])
+    for q in range(2):
+        gates_ready(2, q)
     mates((2, 0), (2, 2))
-    run_chunk([(2, 0), (2, 2)], [(3, lambda: far(1))], False)
+    run_chunk([(2, 0), (2, 2)], 0, experts, [(2, lambda: far(1)), (4, lambda: near(0))])
     mates((2, 1), (2, 3))
-    run_chunk([(2, 1), (2, 3)], [(1, both(2, 0, 2, 2)), (3, lambda: near(0))], False)
+    run_chunk([(2, 1), (2, 3)], 0, experts, [(1, both(2, 0, 2, 2)), (3, lambda: near(1))])
     for o in (1, 3):
         for q in range(2):
             gates_ready(o, q)
     mates((3, 2), (1, 0))
-    run_chunk([(3, 2), (1, 0)], [(1, both(2, 1, 2, 3)), (3, lambda: near(1))], False)
+    run_chunk([(3, 2), (1, 0)], 0, experts, [(1, both(2, 1, 2, 3))])
     mates((3, 3), (1, 1))
-    run_chunk([(3, 3), (1, 1)], [(1, both(3, 2, 1, 0))], False)
+    run_chunk([(3, 3), (1, 1)], 0, experts, [(1, both(3, 2, 1, 0))])
     mates((3, 0), (1, 2))
-    run_chunk([(3, 0), (1, 2)], [(1, both(3, 3, 1, 1))], False)
+    run_chunk([(3, 0), (1, 2)], 0, experts, [(1, both(3, 3, 1, 1))])
     mates((3, 1), (1, 3))
-    run_chunk([(3, 1), (1, 3)], [(1, both(3, 0, 1, 2))], False)
-    both(3, 1, 1, 3)()
+    run_chunk([(3, 1), (1, 3)], 0, experts, [(1, both(3, 0, 1, 2))])
+    run_chunk([(0, 1), (0, 3)], 3, experts, [(3, both(3, 1, 1, 3))])
 
     for p in range(QUARTERS):
         part[0, 0, piece(p)] = partner_sum(0, p)
@@ -233,16 +246,20 @@
     def local_layer(x_loc, ids_loc, gates_loc, hot_loc, hot_g_loc, wg_loc, wu_loc, wd_loc):
         experts, d_model, d_ff = wg_loc.shape
         tokens = x_loc.shape[0]
-        table = gate_table(ids_loc, gates_loc, hot_loc, hot_g_loc, group_size, experts)
+        top_k = ids_loc.shape[1]
+        smem_spec = pl.BlockSpec(memory_space=pltpu.SMEM)
         any_spec = pl.BlockSpec(memory_space=pl.ANY)
         dma = pltpu.SemaphoreType.DMA
         f32, bf16 = jnp.float32, jnp.bfloat16
         return pl.pallas_call(
             moe_kernel,
             out_shape=jax.ShapeDtypeStruct(x_loc.shape, x_loc.dtype),
-            in_specs=[any_spec, pl.BlockSpec(memory_space=pltpu.VMEM), any_spec, any_spec, any_spec],
+            in_specs=[smem_spec, smem_spec] + [any_spec] * 6,
             out_specs=any_spec,
             scratch_shapes=[
+                pltpu.VMEM((top_k, tokens), jnp.int32),
+                pltpu.VMEM((top_k, tokens), f32),
+                pltpu.VMEM((group_size, LANES, tokens), f32),
                 pltpu.VMEM((CHIPS, 2, tokens, d_model), bf16),
                 pltpu.VMEM((experts, d_model, d_ff), bf16),
                 pltpu.VMEM((experts, d_model, d_ff), bf16),
@@ -255,7 +272,7 @@
                 pltpu.VMEM((CHIPS, 2, LANES, tokens), f32),
                 pltpu.VMEM((CHIPS, 2, tokens, LANES), f32),
                 pltpu.VMEM((tokens, d_model), bf16),
-                dma((3 * experts,)), dma,
+                dma((3 * experts,)), dma, dma((2,)),
                 dma((CHIPS, QUARTERS)), dma((CHIPS, QUARTERS)),
                 dma((CHIPS, QUARTERS)), dma((CHIPS, QUARTERS)),
                 dma((CHIPS, 2)), dma((CHIPS, 2)),
@@ -266,7 +283,7 @@
             compiler_params=pltpu.CompilerParams(collective_id=0, has_side_effects=True, vmem_limit_bytes=67_043_328),
             cost_estimate=pl.CostEstimate(flops=100_000_000, bytes_accessed=30_000_000, transcendentals=0),
             name='moe_ring',
-        )(x_loc, table, wg_loc, wu_loc, wd_loc)
+        )(hot_loc, hot_g_loc, x_loc, ids_loc.T, gates_loc.T, wg_loc, wu_loc, wd_loc)
 
     return jax.shard_map(local_layer, mesh=mesh,
                          in_specs=(row_spec, row_spec, row_spec, list_spec, list_spec, expert_spec, expert_spec, expert_spec),

time: 96.9 us -> 91.2 us (0.941)
  Pallas kernels: 92.2 us -> 89 us
  other arithmetic: 2.34 us -> 0 us
    pallas_call x1, Pallas kernels: 92.2 us -> 89 us  [local_layer(): pl.pallas_call(moe_kernel, out_shape=jax.ShapeDtypeStruct(x_loc.shape, x_...]
    reduce_sum x2 -> x0, other arithmetic: 1.61 us -> none  [the longest x1 0.84 us: gate_table(): jnp.sum(jnp.where(ids_loc.T[:, None, :] == expert[None, :, None], gates_l...]
where the time goes in v3:
time: 91.2 us; the launch traced here: 91.1 us
  Pallas kernels  89 us (98%)
  local copies, waits for them, and re-layouts  2.06 us (2%)
    pallas_call x1, Pallas kernels, local_layer(): pl.pallas_call(moe_kernel, out_shape=jax.ShapeDtypeStruct(x_loc.shape, x_...  89 us
    unnamed x1, local copies, waits for them, and re-layouts  2.06 us

profile of v3, /device:TPU:81, one launch (start us, length us, event | category | flops | bytes accessed | tf_op | source)
XLA Modules:
  0.0 91.1 jit_solution(239967586732587368)
XLA Ops:
  0.0 89.0 %moe_ring.1 = bf16[256,1536]{1,0:T(8,128)(2,1)} custom-call(s32[64]{0:T(128)} %hot_ref.1, f32[64]{0:T(128)} %hot_g_ref.1, bf16[256,1536]{1,0:T(8,128)(2,1)} %x_hbm.1, s32[8,256]{1,0:T(8,128)} %bitcast.2, f32[8,256]{1,0:T(8,128)} %bitcast.3, bf16[5,1536,512]{2,1,0:T(8,128)(2,1)} %wg_hbm.1, bf16[5,1536,512]{2,1,0:T(8,128)(2,1)} %wu_hbm.1, ...), custom_call_target="tpu_custom_call" | custom-call | flops 100000000 | bytes 30000000 | tf_op jit(solution)/shard_map/moe_ring/pallas_call | solution.py:254
  89.0 2.1 %copy.10 = bf16[256,1536]{1,0:T(8,128)(2,1)} copy(bf16[256,1536]{1,0:T(8,128)(2,1)} %moe_ring.1) | data formatting | bytes 1572864

commit v4 on v3

--- a/solution.py
+++ b/solution.py
@@ -9,6 +9,7 @@
 
 CHIPS = 4
 QUARTERS = 4
+STRIPS = 8
 LANES = 8
 
 
@@ -30,10 +31,10 @@
         tab_ref[d] = jnp.where(expert == 0, hot, table)
 
 
-def moe_kernel(hot_ref, hot_g_ref, x_hbm, ids_hbm, gates_hbm, wg_hbm, wu_hbm, wd_hbm, out_hbm,
-               ids, gates, tab_ref, xall, wg, wu, wd, part, mate, ring, from_right, from_left, tabs, gcol, stage,
+def moe_kernel(hot_hbm, hot_g_hbm, x_hbm, ids_hbm, gates_hbm, wg_hbm, wu_hbm, wd_hbm, out_hbm,
+               hot_ref, hot_g_ref, ids, gates, tab_ref, xall, wg, wu, wd, part, mate, ring, from_right, from_left, tabs, gcol,
                w_sem, x_sem, in_sem, ag_send, ag_recv, md_send, md_recv, tb_send, tb_recv,
-               pd_send, pd_recv, rs_send, rs_recv, out_sem):
+               pd_send, pd_recv, rs_send, rs_recv):
     experts = wg.shape[0]
     rows = xall.shape[2] // QUARTERS
     me = lax.axis_index('ep')
@@ -45,6 +46,9 @@
     def piece(p):
         return pl.ds(p * rows, rows)
 
+    def strip(i):
+        return pl.ds(i * (rows // 2), rows // 2)
+
     def remote(src, dst, send, recv, device):
         return pltpu.make_async_remote_copy(src_ref=src, dst_ref=dst, send_sem=send, recv_sem=recv,
                                             device_id={'ep': device}, device_id_type=pl.DeviceIdType.MESH)
@@ -55,13 +59,16 @@
         make().start()
         sends.append(make)
 
-    x_copy = pltpu.make_async_copy(x_hbm, xall.at[0, 0], x_sem)
-    x_copy.start()
+    x_copies = [pltpu.make_async_copy(x_hbm.at[strip(i)], xall.at[0, 0, strip(i)], x_sem.at[i])
+                for i in (0, 4, 1, 5, 2, 3, 6, 7)]
+    for copy in x_copies:
+        copy.start()
     w_copies = []
     for e in range(experts):
         for i, (src, dst) in enumerate(((wg_hbm, wg), (wu_hbm, wu), (wd_hbm, wd))):
             w_copies.append(pltpu.make_async_copy(src.at[e], dst.at[e], w_sem.at[3 * e + i]))
-    in_copies = [pltpu.make_async_copy(ids_hbm, ids, in_sem.at[0]), pltpu.make_async_copy(gates_hbm, gates, in_sem.at[1])]
+    in_copies = [pltpu.make_async_copy(ids_hbm, ids, in_sem.at[0]), pltpu.make_async_copy(gates_hbm, gates, in_sem.at[1]),
+                 pltpu.make_async_copy(hot_hbm, hot_ref, in_sem.at[2]), pltpu.make_async_copy(hot_g_hbm, hot_g_ref, in_sem.at[3])]
     for copy in in_copies:
         copy.start()
 
@@ -71,36 +78,41 @@
         pl.semaphore_signal(barrier, inc=1, device_id={'ep': device}, device_id_type=pl.DeviceIdType.MESH)
     pl.semaphore_wait(barrier, len(peers))
 
-    def ring_send(o_src, o_dst, p, device):
-        start(lambda: remote(xall.at[o_src, 0, piece(p)], xall.at[o_dst, 0, piece(p)],
-                             ag_send.at[o_dst, p], ag_recv.at[o_dst, p], device))
-
-    def mate_send(o, p):
-        start(lambda: remote(xall.at[o, 0, piece(p)], xall.at[o, 1, piece(p)],
-                             md_send.at[o, p], md_recv.at[o, p], partner))
-
-    def ring_arrived(o, p):
-        remote(xall.at[o, 0, piece(p)], xall.at[o, 0, piece(p)],
-               ag_send.at[o, p], ag_recv.at[o, p], right).wait_recv()
-        mate_send(o, p)
+    def ring_send(o_src, o_dst, s, device):
+        start(lambda: remote(xall.at[o_src, 0, strip(s)], xall.at[o_dst, 0, strip(s)],
+                             ag_send.at[o_dst, s], ag_recv.at[o_dst, s], device))
+
+    def mate_send(o, s):
+        start(lambda: remote(xall.at[o, 0, strip(s)], xall.at[o, 1, strip(s)],
+                             md_send.at[o, s], md_recv.at[o, s], partner))
+
+    def ring_arrived(o, s):
+        remote(xall.at[o, 0, strip(s)], xall.at[o, 0, strip(s)],
+               ag_send.at[o, s], ag_recv.at[o, s], right).wait_recv()
+        mate_send(o, s)
 
     def mate_arrived(o, p):
-        remote(xall.at[o, 1, piece(p)], xall.at[o, 1, piece(p)],
-               md_send.at[o, p], md_recv.at[o, p], partner).wait_recv()
-
-    x_copy.wait()
-    for p in (0, 1):
-        ring_send(0, 3, p, right)
-        ring_send(0, 1, p + 2, left)
-    for p in range(QUARTERS):
-        mate_send(0, p)
+        for s in (2 * p, 2 * p + 1):
+            remote(xall.at[o, 1, strip(s)], xall.at[o, 1, strip(s)],
+                   md_send.at[o, s], md_recv.at[o, s], partner).wait_recv()
+
+    for i in (0, 1):
+        x_copies[2 * i].wait()
+        ring_send(0, 3, i, right)
+        x_copies[2 * i + 1].wait()
+        ring_send(0, 1, i + 4, left)
+    for copy in x_copies[4:]:
+        copy.wait()
+    for i in range(STRIPS):
+        mate_send(0, i)
     for copy in w_copies:
         copy.start()
     for copy in in_copies:
         copy.wait()
     build_table(ids, gates, hot_ref, hot_g_ref, tab_ref, experts)
     for device, o, q in peers:
-        start(functools.partial(remote, tab_ref.at[device], tabs.at[(CHIPS - o) % CHIPS, q], tb_send.at[o, q],
+        start(functools.partial(remote, tab_ref.at[device, pl.ds(0, experts)],
+                                tabs.at[(CHIPS - o) % CHIPS, q, pl.ds(0, experts)], tb_send.at[o, q],
                                 tb_recv.at[(CHIPS - o) % CHIPS, q], device))
     tabs[0, 0] = tab_ref[me]
 
@@ -108,7 +120,7 @@
 
     def gates_ready(o, q):
         if o or q:
-            remote(tabs.at[o, q], tabs.at[o, q], tb_send.at[o, q], tb_recv.at[o, q], partner).wait_recv()
+            remote(tabs.at[o, q, pl.ds(0, experts)], tabs.at[o, q, pl.ds(0, experts)], tb_send.at[o, q], tb_recv.at[o, q], partner).wait_recv()
         gcol[o, q] = jnp.transpose(tabs[o, q])
 
     def run_chunk(pairs, first, last, hooks):
@@ -166,25 +178,29 @@
         part[o, 0, piece(p)] = total
         start(functools.partial(rs_transfer, o, p, left if goes_left else right))
 
-    def forward(i):
-        ring_arrived(3, i)
-        ring_send(3, 2, i, right)
-        ring_arrived(1, i + 2)
-        ring_send(1, 2, i + 2, left)
-
-    def forward_last():
-        forward(1)
-        for p in (0, 1):
-            ring_send(0, 3, p + 2, right)
-            ring_send(0, 1, p, left)
+    def stage(i):
+        def act():
+            ring_arrived(3, i)
+            ring_send(3, 2, i, right)
+            ring_arrived(1, i + 4)
+            ring_send(1, 2, i + 4, left)
+            for own in ((2,), (3,), (4,), (5, 6, 7))[i]:
+                ring_send(0, 3, own, right)
+                ring_send(0, 1, (own + 4) % STRIPS, left)
+        return act
 
     def far(i):
-        ring_arrived(2, i)
-        ring_arrived(2, i + 2)
+        def act():
+            for s in (2 * i, 2 * i + 1, 2 * i + 4, 2 * i + 5):
+                ring_arrived(2, s)
+        return act
 
     def near(i):
-        ring_arrived(3, i + 2)
-        ring_arrived(1, i)
+        def act():
+            for s in (2 * i, 2 * i + 1):
+                ring_arrived(3, s + 4)
+                ring_arrived(1, s)
+        return act
 
     def both(o1, p1, o2, p2):
         def act():
@@ -199,26 +215,26 @@
     gates_ready(0, 0)
     gates_ready(0, 1)
     mates(*[(0, p) for p in range(QUARTERS)])
-    run_chunk([(0, 0), (0, 2)], 0, experts, [(2, lambda: forward(0)), (4, forward_last)])
-    run_chunk([(0, 1), (0, 3)], 0, 3, [(2, lambda: far(0))])
+    run_chunk([(0, 0), (0, 2)], 0, experts, [(1, stage(0)), (3, stage(1))])
+    run_chunk([(0, 1), (0, 3)], 0, 3, [(1, stage(2)), (2, far(0))])
     for q in range(2):
         gates_ready(2, q)
     mates((2, 0), (2, 2))
-    run_chunk([(2, 0), (2, 2)], 0, experts, [(2, lambda: far(1)), (4, lambda: near(0))])
+    run_chunk([(2, 0), (2, 2)], 0, experts, [(1, stage(3)), (4, far(1))])
     mates((2, 1), (2, 3))
-    run_chunk([(2, 1), (2, 3)], 0, experts, [(1, both(2, 0, 2, 2)), (3, lambda: near(1))])
+    run_chunk([(2, 1), (2, 3)], 0, experts, [(1, both(2, 0, 2, 2)), (3, near(0))])
     for o in (1, 3):
         for q in range(2):
             gates_ready(o, q)
     mates((3, 2), (1, 0))
-    run_chunk([(3, 2), (1, 0)], 0, experts, [(1, both(2, 1, 2, 3))])
+    run_chunk([(3, 2), (1, 0)], 0, experts, [(1, both(2, 1, 2, 3)), (2, near(1))])
     mates((3, 3), (1, 1))
     run_chunk([(3, 3), (1, 1)], 0, experts, [(1, both(3, 2, 1, 0))])
     mates((3, 0), (1, 2))
     run_chunk([(3, 0), (1, 2)], 0, experts, [(1, both(3, 3, 1, 1))])
     mates((3, 1), (1, 3))
     run_chunk([(3, 1), (1, 3)], 0, experts, [(1, both(3, 0, 1, 2))])
-    run_chunk([(0, 1), (0, 3)], 3, experts, [(3, both(3, 1, 1, 3))])
+    run_chunk([(0, 1), (0, 3)], 3, experts, [(4, both(3, 1, 1, 3))])
 
     for p in range(QUARTERS):
         part[0, 0, piece(p)] = partner_sum(0, p)
@@ -227,14 +243,9 @@
         rs_transfer(3, p, left).wait_recv()
         rs_transfer(1, p, left).wait_recv()
         total = part[0, 0, piece(p)] + from_right[piece(p)] + from_left[piece(p)]
-        stage[piece(p)] = total.astype(stage.dtype)
-        copy = pltpu.make_async_copy(stage.at[piece(p)], out_hbm.at[piece(p)], out_sem.at[p])
-        copy.start()
-        out_copies.append(copy)
+        out_hbm[piece(p)] = total.astype(out_hbm.dtype)
     for make in sends:
         make().wait_send()
-    for copy in out_copies:
-        copy.wait()
 
 
 def solution(mesh):
@@ -247,16 +258,18 @@
         experts, d_model, d_ff = wg_loc.shape
         tokens = x_loc.shape[0]
         top_k = ids_loc.shape[1]
-        smem_spec = pl.BlockSpec(memory_space=pltpu.SMEM)
+        hot_rows = hot_loc.shape[0]
         any_spec = pl.BlockSpec(memory_space=pl.ANY)
         dma = pltpu.SemaphoreType.DMA
         f32, bf16 = jnp.float32, jnp.bfloat16
         return pl.pallas_call(
             moe_kernel,
-            out_shape=jax.ShapeDtypeStruct(x_loc.shape, x_loc.dtype),
-            in_specs=[smem_spec, smem_spec] + [any_spec] * 6,
-            out_specs=any_spec,
+            out_shape=pltpu.VMEM(x_loc.shape, x_loc.dtype),
+            in_specs=[any_spec] * 8,
+            out_specs=pl.BlockSpec(memory_space=pltpu.VMEM),
             scratch_shapes=[
+                pltpu.SMEM((hot_rows,), jnp.int32),
+                pltpu.SMEM((hot_rows,), f32),
                 pltpu.VMEM((top_k, tokens), jnp.int32),
                 pltpu.VMEM((top_k, tokens), f32),
                 pltpu.VMEM((group_size, LANES, tokens), f32),
@@ -271,16 +284,14 @@
                 pltpu.VMEM((tokens, d_model), f32),
                 pltpu.VMEM((CHIPS, 2, LANES, tokens), f32),
                 pltpu.VMEM((CHIPS, 2, tokens, LANES), f32),
-                pltpu.VMEM((tokens, d_model), bf16),
-                dma((3 * experts,)), dma, dma((2,)),
-                dma((CHIPS, QUARTERS)), dma((CHIPS, QUARTERS)),
-                dma((CHIPS, QUARTERS)), dma((CHIPS, QUARTERS)),
+                dma((3 * experts,)), dma((STRIPS,)), dma((4,)),
+                dma((CHIPS, STRIPS)), dma((CHIPS, STRIPS)),
+                dma((CHIPS, STRIPS)), dma((CHIPS, STRIPS)),
                 dma((CHIPS, 2)), dma((CHIPS, 2)),
                 dma((CHIPS, QUARTERS)), dma((CHIPS, QUARTERS)),
                 dma((CHIPS, QUARTERS)), dma((CHIPS, QUARTERS)),
-                dma((QUARTERS,)),
             ],
-            compiler_params=pltpu.CompilerParams(collective_id=0, has_side_effects=True, vmem_limit_bytes=67_043_328),
+            compiler_params=pltpu.CompilerParams(collective_id=0, has_side_effects=True, vmem_limit_bytes=62_000_000),
             cost_estimate=pl.CostEstimate(flops=100_000_000, bytes_accessed=30_000_000, transcendentals=0),
             name='moe_ring',
         )(hot_loc, hot_g_loc, x_loc, ids_loc.T, gates_loc.T, wg_loc, wu_loc, wd_loc)

time: 91.2 us -> 87 us (0.954)
  Pallas kernels: 89 us -> 86 us
  local copies, waits for them, and re-layouts: 2.06 us -> 0.88 us
    pallas_call x1, Pallas kernels: 89 us -> 86 us  [local_layer(): pl.pallas_call(moe_kernel, out_shape=pltpu.VMEM(x_loc.shape, x_loc.dtype)...]
    unnamed x1, local copies, waits for them, and re-layouts: 2.06 us -> 0.88 us
where the time goes in v4:
time: 87 us; the launch traced here: 86.9 us
  Pallas kernels  86 us (99%)
  local copies, waits for them, and re-layouts  0.88 us (1%)
    pallas_call x1, Pallas kernels, local_layer(): pl.pallas_call(moe_kernel, out_shape=pltpu.VMEM(x_loc.shape, x_loc.dtype)...  86 us

profile of v4, /device:TPU:81, one launch (start us, length us, event | category | flops | bytes accessed | tf_op | source)
XLA Modules:
  0.0 86.9 jit_solution(6287287974377001308)
XLA Ops:
  0.0 86.0 %moe_ring.1 = bf16[256,1536]{1,0:T(8,128)(2,1)S(1)} custom-call(s32[64]{0:T(128)} %hot_hbm.1, f32[64]{0:T(128)} %hot_g_hbm.1, bf16[256,1536]{1,0:T(8,128)(2,1)} %x_hbm.1, s32[8,256]{1,0:T(8,128)} %bitcast.2, f32[8,256]{1,0:T(8,128)} %bitcast.3, bf16[5,1536,512]{2,1,0:T(8,128)(2,1)} %wg_hbm.1, bf16[5,1536,512]{2,1,0:T(8,128)(2,1)} %wu_hbm.1, ...), custom_call_target="tpu_custom_call" | custom-call | flops 100000000 | bytes 30000000 | tf_op jit(solution)/shard_map/moe_ring/pallas_call | solution.py:265
  86.0 0.9 %copy.10 = bf16[256,1536]{1,0:T(8,128)(2,1)} copy(bf16[256,1536]{1,0:T(8,128)(2,1)S(1)} %moe_ring.1) | data formatting | bytes 1572864

commit v5 on v4

--- a/solution.py
+++ b/solution.py
@@ -123,15 +123,21 @@
             remote(tabs.at[o, q, pl.ds(0, experts)], tabs.at[o, q, pl.ds(0, experts)], tb_send.at[o, q], tb_recv.at[o, q], partner).wait_recv()
         gcol[o, q] = jnp.transpose(tabs[o, q])
 
-    def run_chunk(pairs, first, last, hooks):
+    def run_chunk(pairs, first, last, hooks, unroll=False):
         groups = [(o, q, p) for o, p in pairs for q in range(2)]
         if first == 0:
             for o, q, p in groups:
                 part[o, q, piece(p)] = jnp.zeros((rows, part.shape[3]), jnp.float32)
 
+        def call_hooks(at):
+            for step, hook in hooks:
+                if not unroll:
+                    pl.when(at == step)(hook)
+                elif at == step:
+                    hook()
+
         def body(e, _):
-            for step, hook in hooks:
-                pl.when(e == step)(hook)
+            call_hooks(e)
             if (pairs, first) == ([(0, 0), (0, 2)], 0):
                 for i in range(3):
                     ref = (wg, wu, wd)[i]
@@ -144,6 +150,8 @@
                 a = jnp.dot(x, wg[e, :, cols], preferred_element_type=jnp.float32)
                 b = jnp.dot(x, wu[e, :, cols], preferred_element_type=jnp.float32)
                 hidden.append((a * jax.nn.sigmoid(a) * b).astype(jnp.bfloat16))
+            if unroll:
+                call_hooks(e + 0.5)
             u = jnp.concatenate(hidden, axis=1)
             weight = [jnp.sum(jnp.where(lane == e, gcol[o, q, piece(p)], 0.0), axis=1, keepdims=True)
                       for o, q, p in groups]
@@ -156,7 +164,11 @@
                     part[o, q, piece(p), cols] += jnp.where(weight[i] != 0, weight[i] * hi, 0.0)
             return 0
 
-        lax.fori_loop(first, last, body, 0)
+        if unroll:
+            for e in range(first, last):
+                body(e, 0)
+        else:
+            lax.fori_loop(first, last, body, 0)
         for o, p in pairs if last == experts else ():
             start(functools.partial(remote, part.at[o, 1, piece(p)], mate.at[o, piece(p)],
                                     pd_send.at[o, p], pd_recv.at[o, p], partner))
@@ -216,25 +228,26 @@
     gates_ready(0, 1)
     mates(*[(0, p) for p in range(QUARTERS)])
     run_chunk([(0, 0), (0, 2)], 0, experts, [(1, stage(0)), (3, stage(1))])
-    run_chunk([(0, 1), (0, 3)], 0, 3, [(1, stage(2)), (2, far(0))])
+    run_chunk([(0, 1), (0, 3)], 0, 2, [(1, stage(2))])
+    far(0)()
     for q in range(2):
         gates_ready(2, q)
     mates((2, 0), (2, 2))
-    run_chunk([(2, 0), (2, 2)], 0, experts, [(1, stage(3)), (4, far(1))])
+    run_chunk([(2, 0), (2, 2)], 0, experts, [(1, stage(3)), (4, far(1))], True)
     mates((2, 1), (2, 3))
-    run_chunk([(2, 1), (2, 3)], 0, experts, [(1, both(2, 0, 2, 2)), (3, near(0))])
+    run_chunk([(2, 1), (2, 3)], 0, experts, [(1.5, both(2, 0, 2, 2)), (3, near(0))], True)
     for o in (1, 3):
         for q in range(2):
             gates_ready(o, q)
     mates((3, 2), (1, 0))
-    run_chunk([(3, 2), (1, 0)], 0, experts, [(1, both(2, 1, 2, 3)), (2, near(1))])
+    run_chunk([(3, 2), (1, 0)], 0, experts, [(1.5, both(2, 1, 2, 3)), (2, near(1))], True)
     mates((3, 3), (1, 1))
-    run_chunk([(3, 3), (1, 1)], 0, experts, [(1, both(3, 2, 1, 0))])
+    run_chunk([(3, 3), (1, 1)], 0, experts, [(1.5, both(3, 2, 1, 0))], True)
     mates((3, 0), (1, 2))
-    run_chunk([(3, 0), (1, 2)], 0, experts, [(1, both(3, 3, 1, 1))])
+    run_chunk([(3, 0), (1, 2)], 0, experts, [(1.5, both(3, 3, 1, 1))], True)
     mates((3, 1), (1, 3))
     run_chunk([(3, 1), (1, 3)], 0, experts, [(1, both(3, 0, 1, 2))])
-    run_chunk([(0, 1), (0, 3)], 3, experts, [(4, both(3, 1, 1, 3))])
+    run_chunk([(0, 1), (0, 3)], 2, experts, [(4, both(3, 1, 1, 3))])
 
     for p in range(QUARTERS):
         part[0, 0, piece(p)] = partner_sum(0, p)

time: 87 us -> 86.3 us (level)
  no operation moved by 1% of the time
where the time goes in v5:
time: 86.3 us; the launch traced here: 86.2 us
  Pallas kernels  85.3 us (99%)
  local copies, waits for them, and re-layouts  0.88 us (1%)
    pallas_call x1, Pallas kernels, local_layer(): pl.pallas_call(moe_kernel, out_shape=pltpu.VMEM(x_loc.shape, x_loc.dtype)...  85.3 us

profile of v5, /device:TPU:81, one launch (start us, length us, event | category | flops | bytes accessed | tf_op | source)
XLA Modules:
  0.0 86.2 jit_solution(9076853127630889781)
XLA Ops:
  0.0 85.3 %moe_ring.1 = bf16[256,1536]{1,0:T(8,128)(2,1)S(1)} custom-call(s32[64]{0:T(128)} %hot_hbm.1, f32[64]{0:T(128)} %hot_g_hbm.1, bf16[256,1536]{1,0:T(8,128)(2,1)} %x_hbm.1, s32[8,256]{1,0:T(8,128)} %bitcast.2, f32[8,256]{1,0:T(8,128)} %bitcast.3, bf16[5,1536,512]{2,1,0:T(8,128)(2,1)} %wg_hbm.1, bf16[5,1536,512]{2,1,0:T(8,128)(2,1)} %wu_hbm.1, ...), custom_call_target="tpu_custom_call" | custom-call | flops 100000000 | bytes 30000000 | tf_op jit(solution)/shard_map/moe_ring/pallas_call | solution.py:278
  85.3 0.9 %copy.10 = bf16[256,1536]{1,0:T(8,128)(2,1)} copy(bf16[256,1536]{1,0:T(8,128)(2,1)S(1)} %moe_ring.1) | data formatting | bytes 1572864

commit v6 on v5

--- a/solution.py
+++ b/solution.py
@@ -53,7 +53,7 @@
         return pltpu.make_async_remote_copy(src_ref=src, dst_ref=dst, send_sem=send, recv_sem=recv,
                                             device_id={'ep': device}, device_id_type=pl.DeviceIdType.MESH)
 
-    sends = []
+    sends, sums_sent = [], []
 
     def start(make):
         make().start()
@@ -188,7 +188,9 @@
             rs_transfer(2, p, left).wait_recv()
             total = total + ring[piece(p)]
         part[o, 0, piece(p)] = total
-        start(functools.partial(rs_transfer, o, p, left if goes_left else right))
+        make = functools.partial(rs_transfer, o, p, left if goes_left else right)
+        make().start()
+        sums_sent.append(make)
 
     def stage(i):
         def act():
@@ -252,12 +254,14 @@
     for p in range(QUARTERS):
         part[0, 0, piece(p)] = partner_sum(0, p)
     out_copies = []
+    for make in sends + sums_sent[:8]:
+        make().wait_send()
     for p in (0, 2, 1, 3):
         rs_transfer(3, p, left).wait_recv()
         rs_transfer(1, p, left).wait_recv()
         total = part[0, 0, piece(p)] + from_right[piece(p)] + from_left[piece(p)]
         out_hbm[piece(p)] = total.astype(out_hbm.dtype)
-    for make in sends:
+    for make in sums_sent[8:]:
         make().wait_send()
 
 

time: 86.3 us -> 86.1 us (level)
  no operation moved by 1% of the time
where the time goes in v6:
time: 86.1 us; the launch traced here: 86 us
  Pallas kernels  85.2 us (99%)
  local copies, waits for them, and re-layouts  0.88 us (1%)
    pallas_call x1, Pallas kernels, local_layer(): pl.pallas_call(moe_kernel, out_shape=pltpu.VMEM(x_loc.shape, x_loc.dtype)...  85.2 us

profile of v6, /device:TPU:81, one launch (start us, length us, event | category | flops | bytes accessed | tf_op | source)
XLA Modules:
  0.0 86.0 jit_solution(5777932251422713403)
XLA Ops:
  0.0 85.2 %moe_ring.1 = bf16[256,1536]{1,0:T(8,128)(2,1)S(1)} custom-call(s32[64]{0:T(128)} %hot_hbm.1, f32[64]{0:T(128)} %hot_g_hbm.1, bf16[256,1536]{1,0:T(8,128)(2,1)} %x_hbm.1, s32[8,256]{1,0:T(8,128)} %bitcast.2, f32[8,256]{1,0:T(8,128)} %bitcast.3, bf16[5,1536,512]{2,1,0:T(8,128)(2,1)} %wg_hbm.1, bf16[5,1536,512]{2,1,0:T(8,128)(2,1)} %wu_hbm.1, ...), custom_call_target="tpu_custom_call" | custom-call | flops 100000000 | bytes 30000000 | tf_op jit(solution)/shard_map/moe_ring/pallas_call | solution.py:282
  85.2 0.9 %copy.10 = bf16[256,1536]{1,0:T(8,128)(2,1)} copy(bf16[256,1536]{1,0:T(8,128)(2,1)S(1)} %moe_ring.1) | data formatting | bytes 1572864
